TPU v7x, 32 devices: a whole 2x2x4 slice. The times are simulated.
32 devices in a mesh: dp: 16 (over z, x, core), mp: 2 (over y).
Axes of the slice: x: 2, y: 2, z: 4, core: 2. Of those that a mesh axis runs over, the one named last changes fastest.
Arguments:
- inputs_store: bfloat16 [512, 128], replicated, may hold values from -6 to 6
- window: int32 [16], replicated, may hold values from 0 to 511
- targets_store: bfloat16 [512, 4096], P(None, ('dp', 'mp')), may hold values from -6 to 6
- jac_store: bfloat16 [512, 4096, 128], P(None, ('dp', 'mp')), may hold values from -4 to 4
- first_weight: bfloat16 [128, 1024], replicated, may hold values from -0.5 to 0.5
- first_bias: bfloat16 [1024], replicated, may hold values from -3 to 3
- hidden_weight: bfloat16 [1024, 1024], P(None, 'mp'), may hold values from -0.1875 to 0.1875
- hidden_bias: bfloat16 [1024], P('mp'), may hold values from -3 to 3
- decoder_weight: bfloat16 [4096, 1024], P(('dp', 'mp')), may hold values from -0.1875 to 0.1875
Outputs:
- first_weights: float32 [128, 1024], replicated
- first_biases: float32 [1024], replicated
- hidden_weights: float32 [1024, 1024], P(None, 'mp')
- hidden_biases: float32 [1024], P('mp')
- decoder_grad: float32 [4096, 1024], P(('dp', 'mp'))
Inputs may be any that keep to these rules, and one draw needn't show every extreme that they name: `window`: indices of stored samples; an index may repeat.
All inputs are finite; a program needn't handle non-finite values.
Results may differ from a plain program's by a relative error of at most 0.011.
Values may be sent and summed in bfloat16 or wider, within the bound.
No kernel may reach another device: no remote copies, remote signals or barrier semaphores. Data moves between devices by JAX's collectives and lax.ppermute only.
A program may use at most 64 MiB of HBM per device.

v0:
```python
import jax
import jax.numpy as jnp
from jax import lax
from jax.sharding import PartitionSpec as P


def on_device(
    inputs_store,
    window,
    targets_store,
    jac_store,
    first_weight,
    first_bias,
    hidden_weight,
    hidden_bias,
    decoder_weight,
):
    each_count = window.shape[0] // lax.axis_size("dp")
    jac_window = jac_store[window]
    target_window = targets_store[window]
    jac_mine, target_mine = (
        lax.all_to_all(jac_window, "dp", split_axis=0, concat_axis=1, tiled=True),
        lax.all_to_all(target_window, "dp", split_axis=0, concat_axis=1, tiled=True),
    )
    mine_index = lax.dynamic_slice_in_dim(window, lax.axis_index("dp") * each_count, each_count)
    inputs = inputs_store[mine_index]
    weight_one = first_weight.astype(jnp.float32)
    first_pre = jnp.dot(
        inputs, first_weight, preferred_element_type=jnp.float32
    ) + first_bias.astype(jnp.float32)
    first_act = jnp.tanh(first_pre)
    first_slope = 1.0 - first_act * first_act
    first_tan = (first_slope[:, None, :] * weight_one[None]).astype(jnp.bfloat16)
    first_round = first_act.astype(jnp.bfloat16)
    hidden_lin = jnp.einsum(
        "srh,hk->srk", first_tan, hidden_weight, preferred_element_type=jnp.float32
    )
    hidden_pre = jnp.dot(
        first_round, hidden_weight, preferred_element_type=jnp.float32
    ) + hidden_bias.astype(jnp.float32)
    hidden_act = jnp.tanh(hidden_pre)
    hidden_slope = 1.0 - hidden_act * hidden_act
    hidden_tangent = (hidden_slope[:, None, :] * hidden_lin).astype(jnp.bfloat16)
    hidden_rounded_state = hidden_act.astype(jnp.bfloat16)
    act_all, tangent_full_rows = (
        lax.all_gather(hidden_rounded_state, "mp", axis=1, tiled=True),
        lax.all_gather(hidden_tangent, "mp", axis=2, tiled=True),
    )
    decoder_full_rows = lax.all_gather(decoder_weight, "dp", axis=0, tiled=True)
    outputs_net = jnp.einsum(
        "sk,ok->so", act_all, decoder_full_rows, preferred_element_type=jnp.float32
    )
    jacobian_predicted = jnp.einsum(
        "mvn,an->mav", tangent_full_rows, decoder_full_rows, preferred_element_type=jnp.float32
    )
    output_residual = (outputs_net - target_mine.astype(jnp.float32)).astype(jnp.bfloat16)
    jacobian_residual = (jacobian_predicted - jac_mine.astype(jnp.float32)).astype(jnp.bfloat16)
    decoder_grad = lax.psum_scatter(
        jnp.einsum("qi,qm->im", output_residual, act_all, preferred_element_type=jnp.float32)
        + jnp.einsum(
            "hzy,hym->zm", jacobian_residual, tangent_full_rows, preferred_element_type=jnp.float32
        ),
        "dp",
        scatter_dimension=0,
        tiled=True,
    )
    act_partial = jnp.einsum(
        "so,oh->sh", output_residual, decoder_full_rows, preferred_element_type=jnp.float32
    )
    tan_partial = jnp.einsum(
        "lud,uf->ldf", jacobian_residual, decoder_full_rows, preferred_element_type=jnp.float32
    )
    act_back, tan_back = (
        lax.psum_scatter(
            act_partial.astype(jnp.bfloat16), "mp", scatter_dimension=1, tiled=True
        ).astype(jnp.float32),
        lax.psum_scatter(
            tan_partial.astype(jnp.bfloat16), "mp", scatter_dimension=2, tiled=True
        ).astype(jnp.float32),
    )
    lin_back = tan_back * hidden_slope[:, None, :]
    pre_back = act_back * hidden_slope - 2.0 * hidden_act * hidden_slope * jnp.sum(
        tan_back * hidden_lin, axis=1
    )
    lin_round = lin_back.astype(jnp.bfloat16)
    pre_round = pre_back.astype(jnp.bfloat16)
    hidden_grad = jnp.einsum(
        "sh,sk->hk", first_round, pre_round, preferred_element_type=jnp.float32
    ) + jnp.einsum("srh,srk->hk", first_tan, lin_round, preferred_element_type=jnp.float32)
    hidden_bgrad = jnp.sum(pre_back, axis=0)
    tan_lower = jnp.einsum(
        "srk,hk->srh", lin_round, hidden_weight, preferred_element_type=jnp.float32
    )
    act_lower = jnp.einsum(
        "sk,hk->sh", pre_round, hidden_weight, preferred_element_type=jnp.float32
    )
    pre_lower = act_lower * first_slope - 2.0 * first_act * first_slope * jnp.sum(
        tan_lower * weight_one[None], axis=1
    )
    weight_part = jnp.einsum(
        "sr,sh->rh", inputs.astype(jnp.float32), pre_lower, precision=lax.Precision.HIGHEST
    ) + jnp.sum(tan_lower * first_slope[:, None, :], axis=0)
    bias_part = jnp.sum(pre_lower, axis=0)
    weight_mid, bias_mid = (
        lax.psum(weight_part.astype(jnp.bfloat16), "mp").astype(jnp.float32),
        lax.psum(bias_part.astype(jnp.bfloat16), "mp").astype(jnp.float32),
    )
    first_weights, first_biases, hidden_weights, hidden_biases = lax.psum(
        (weight_mid, bias_mid, hidden_grad, hidden_bgrad), "dp"
    )
    return (first_weights, first_biases, hidden_weights, hidden_biases, decoder_grad)


def solution(mesh):
    placed = (
        P(),
        P(),
        P(None, ("dp", "mp")),
        P(None, ("dp", "mp"), None),
        P(),
        P(),
        P(None, "mp"),
        P("mp"),
        P(("dp", "mp"), None),
    )
    return jax.shard_map(
        on_device,
        mesh=mesh,
        in_specs=placed,
        out_specs=(P(), P(), P(None, "mp"), P("mp"), P(("dp", "mp"), None)),
        check_vma=False,
    )
```

profile of v0, /device:TPU:0, one launch (start us, length us, event | category | flops | bytes accessed | tf_op | source)
XLA Modules:
  0.0 348.1 jit_solution(14651161969415206212)
XLA Ops:
  8.6 1.5 gather_fusion
  10.7 7.4 %all-to-all-start = ((bf16[16,1,128]{2,1,0:T(2,128)(2,1)}), bf16[16,1,128]{2,1,0:T(2,128)(2,1)S(1)}, u32[]{:S(2)}, u32[]{:S(2)}) async-start(bf16[16,1,128]{2,1,0:T(2,128)(2,1)} %copy.16), calls=%async_computation | async-start | bytes 16384 | tf_op jit(solution)/shard_map/all_to_all | solution.py:23
  18.1 1.2 dynamic_slice.3
  22.4 7.2 %gather_fusion.1 = bf16[16,128,128]{2,1,0:T(8,128)(2,1)} fusion(bf16[512,128,128]{2,1,0:T(8,128)(2,1)} %param.12, s32[1024]{0:T(1024)S(1)} %pad_clamp_fusion), kind=kCustom, calls=%fused_computation.1 | custom fusion | bytes 1048640 | tf_op jit(solution)/shard_map/gather | solution.py:19
  29.6 6.0 %all-to-all-start.1 = ((bf16[16,128,128]{2,1,0:T(8,128)(2,1)}), bf16[16,128,128]{2,1,0:T(8,128)(2,1)S(1)}, u32[]{:S(2)}, u32[]{:S(2)}) async-start(bf16[16,128,128]{2,1,0:T(8,128)(2,1)} %gather_fusion.1), calls=%async_computation.1 | async-start | bytes 1048576 | tf_op jit(solution)/shard_map/all_to_all | solution.py:22
  37.3 4.4 %all-gather.2 = bf16[2,1,512]{2,1,0:T(2,128)(2,1)S(1)} all-gather(bf16[1,1,512]{2,1,0:T(2,128)(2,1)S(1)} %reshape.173), channel_id=2, replica_groups=mesh['dp'=16,'mp'=2] {'mp'}, dimensions={0}, use_global_device_ids=true | all-gather | bytes 3072 | tf_op jit(solution)/shard_map/all_gather | solution.py:46
  41.7 2.0 multiply_convert_fusion
  43.7 5.6 %all-gather.1 = bf16[128,1024]{1,0:T(8,128)(2,1)S(1)} all-gather(bf16[128,512]{1,0:T(8,128)(2,1)S(1)} %get-tuple-element.30), channel_id=3, replica_groups=mesh['dp'=16,'mp'=2] {'mp'}, dimensions={1}, use_global_device_ids=true | all-gather | bytes 393216 | tf_op jit(solution)/shard_map/all_gather | solution.py:47
  49.3 6.6 %all-to-all-done.1 = bf16[16,128,128]{2,1,0:T(8,128)(2,1)S(1)} async-done(((bf16[16,128,128]{2,1,0:T(8,128)(2,1)}), bf16[16,128,128]{2,1,0:T(8,128)(2,1)S(1)}, u32[]{:S(2)}, u32[]{:S(2)}) %all-to-all-start.1) | async-done | bytes 524320 | tf_op jit(solution)/shard_map/all_to_all | solution.py:22
  56.4 13.1 %all-gather.5.cloned.1.call-done = bf16[2048,1024]{1,0:T(8,128)(2,1)} async-done(((bf16[128,1024]{1,0:T(8,128)(2,1)}), bf16[2048,1024]{1,0:T(8,128)(2,1)}) %all-gather.5.cloned.1.call-update) | async-done | bytes 4194320 | tf_op jit(solution)/shard_map/all_gather | solution.py:49
  69.4 3.5 %fusion.26 = f32[1,2048]{1,0:T(1,128)S(1)} fusion(bf16[1024,1]{0,1:T(2,128)(2,1)S(1)} %bitcast.62, bf16[2048,1024]{1,0:T(8,128)(2,1)} %all-gather.5.cloned.1.call-done), kind=kOutput, calls=%fused_computation.48 | convolution fusion | flops 4194304 | bytes 4204544 | tf_op jit(solution)/shard_map/sk,ok->so/dot_general | solution.py:50
  74.6 3.8 %fusion.1 = bf16[2048,128]{0,1:T(8,128)(2,1)S(1)} fusion(f32[2048,128]{0,1:T(8,128)S(1)} %copy.18, bf16[128,1024]{1,0:T(8,128)(2,1)S(1)} %all-gather.1, bf16[2048,1024]{1,0:T(8,128)(2,1)} %all-gather.5.cloned.1.call-done), kind=kOutput, calls=%fused_computation.5 | convolution fusion | flops 537395200 | bytes 6029312 | tf_op jit(solution)/shard_map/mvn,an->mav/dot_general | solution.py:53
  78.6 1.4 fusion.2
  80.8 4.4 %reduce-scatter.10.cloned.1.call-done = bf16[512,1]{1,0:T(8,128)(2,1)} async-done(((bf16[1024,1]{1,0:T(8,128)(2,1)}), bf16[512,1]{1,0:T(8,128)(2,1)}) %reduce-scatter.10.cloned.1.call-update) | async-done | bytes 1040
  86.2 13.6 %reduce-scatter.6.cloned.1.call-done = bf16[1,128,512]{2,1,0:T(8,128)(2,1)} async-done(((bf16[1,128,1024]{2,1,0:T(8,128)(2,1)}), bf16[1,128,512]{2,1,0:T(8,128)(2,1)}) %reduce-scatter.6.cloned.1.call-update) | async-done | bytes 131088 | tf_op jit(solution)/shard_map/reduce_scatter | solution.py:77
  101.3 1.4 fusion.4
  103.7 1.8 multiply_add_fusion.1
  105.6 4.5 %multiply_add_fusion = f32[2048,1024]{1,0:T(8,128)} fusion(bf16[2048,128]{0,1:T(8,128)(2,1)S(1)} %fusion.1, bf16[128,1024]{1,0:T(8,128)(2,1)S(1)} %all-gather.1, f32[1024]{0:T(1024)S(1)} %convert.21, f32[2048]{0:T(1024)S(1)} %get-tuple-element.19), kind=kOutput, calls=%fused_computation.2 | convolution fusion | flops 541065216 | bytes 9187328 | tf_op jit(solution)/shard_map/hzy,hym->zm/dot_general | solution.py:60
  110.1 4.9 %psum.44 = bf16[1024]{0:T(1024)(128)(2,1)S(1)} all-reduce(bf16[1024]{0:T(1024)(128)(2,1)S(1)} %get-tuple-element.25), channel_id=1, replica_groups=mesh['dp'=16,'mp'=2] {'mp'}, use_global_device_ids=true, to_apply=%region_6.0 | all-reduce | flops 1024 | bytes 4096 | tf_op jit(solution)/shard_map/psum | solution.py:106
  115.1 12.0 %all-reduce.5.cloned.1.call-done = bf16[128,1024]{1,0:T(8,128)(2,1)} async-done(((bf16[128,1024]{1,0:T(8,128)(2,1)}), bf16[128,1024]{1,0:T(8,128)(2,1)}) %all-reduce.5.cloned.1.call-update) | async-done | bytes 262160 | tf_op jit(solution)/shard_map/psum | solution.py:105
  127.1 70.9 %all-reduce.8 = (f32[128,1024]{1,0:T(8,128)}, f32[1024]{0:T(1024)}, f32[512]{0:T(512)}) all-reduce(bf16[128,1024]{1,0:T(8,128)(2,1)} %all-reduce.5.cloned.1.call-done, bf16[1024]{0:T(1024)(128)(2,1)S(1)} %psum.44, f32[512]{0:T(512)S(1)} %bitcast.67), channel_id=1, replica_groups=mesh['dp'=16,'mp'=2] {'dp'}, use_global_device_ids=true, to_apply=%region_5.0 | all-reduce | flops 132608 | bytes 796672 | tf_op jit(solution)/shard_map/psum | solution.py:108
  198.0 33.0 %all-reduce.7.cloned.1.call-done = f32[1024,512]{1,0:T(8,128)} async-done(((f32[1024,512]{1,0:T(8,128)}), f32[1024,512]{1,0:T(8,128)}) %all-reduce.7.cloned.1.call-update) | async-done | bytes 2097168 | tf_op jit(solution)/shard_map/psum | solution.py:108
  231.0 107.3 %reduce-scatter.8.cloned.1.call-done = f32[128,1024]{1,0:T(8,128)} async-done(((f32[2048,1024]{1,0:T(8,128)}), f32[128,1024]{1,0:T(8,128)}) %reduce-scatter.8.cloned.1.call-update) | async-done | bytes 524304 | tf_op jit(solution)/shard_map/reduce_scatter | solution.py:58
  338.2 3.1 copy.29
  (58 shorter events, 11.1 us)
Async XLA Ops:
  7.2 29.2 %copy-start = (bf16[1024,512]{1,0:T(8,128)(2,1)S(1)}, bf16[1024,512]{1,0:T(8,128)(2,1)}, u32[]{:S(2)}) copy-start(bf16[1024,512]{1,0:T(8,128)(2,1)} %param.15) | copy-start | bytes 3145732
  7.2 62.2 %all-gather.5.cloned.1.call-start = ((), (), s32[]{:S(2)}) async-start(), calls=%async_computation.5 | async-start | bytes 4456448 | tf_op jit(solution)/shard_map/all_gather | solution.py:49
  10.7 18.9 %all-to-all-start = ((bf16[16,1,128]{2,1,0:T(2,128)(2,1)}), bf16[16,1,128]{2,1,0:T(2,128)(2,1)S(1)}, u32[]{:S(2)}, u32[]{:S(2)}) async-start(bf16[16,1,128]{2,1,0:T(2,128)(2,1)} %copy.16), calls=%async_computation | async-start | bytes 16384 | tf_op jit(solution)/shard_map/all_to_all | solution.py:23
  29.6 26.3 %all-to-all-start.1 = ((bf16[16,128,128]{2,1,0:T(8,128)(2,1)}), bf16[16,128,128]{2,1,0:T(8,128)(2,1)S(1)}, u32[]{:S(2)}, u32[]{:S(2)}) async-start(bf16[16,128,128]{2,1,0:T(8,128)(2,1)} %gather_fusion.1), calls=%async_computation.1 | async-start | bytes 1048576 | tf_op jit(solution)/shard_map/all_to_all | solution.py:22
  35.6 49.6 %reduce-scatter.10.cloned.1.call-start = ((), (), s32[]{:S(2)}) async-start(), calls=%async_computation.10 | async-start | bytes 393216
  69.4 3.6 %copy-start.1 = (bf16[2048,1024]{1,0:T(8,128)(2,1)S(1)}, bf16[2048,1024]{1,0:T(8,128)(2,1)}, u32[]{:S(2)}) copy-start(bf16[2048,1024]{1,0:T(8,128)(2,1)} %all-gather.5.cloned.1.call-done) | copy-start | bytes 12582916
  74.6 25.3 %reduce-scatter.6.cloned.1.call-start = ((), (), s32[]{:S(2)}) async-start(), calls=%async_computation.6 | async-start | bytes 393216 | tf_op jit(solution)/shard_map/reduce_scatter | solution.py:77
  74.6 3.9 %copy-start.2 = (bf16[2048,1024]{1,0:T(8,128)(2,1)S(1)}, bf16[2048,1024]{1,0:T(8,128)(2,1)}, u32[]{:S(2)}) copy-start(bf16[2048,1024]{1,0:T(8,128)(2,1)} %all-gather.5.cloned.1.call-done) | copy-start | bytes 12582916
  78.5 21.4 %copy-start.5 = (f32[128,512]{1,0:T(8,128)S(1)}, f32[128,512]{1,0:T(8,128)}, u32[]{:S(2)}) copy-start(f32[128,512]{1,0:T(8,128)} %get-tuple-element.31) | copy-start | bytes 786436
  78.5 22.4 %copy-start.7 = (bf16[512]{0:T(512)(128)(2,1)S(1)}, bf16[512]{0:T(512)(128)(2,1)}, u32[]{:S(2)}) copy-start(bf16[512]{0:T(512)(128)(2,1)} %param.16) | copy-start | bytes 3076
  78.5 22.8 %copy-start.3 = (bf16[128,1024]{1,0:T(8,128)(2,1)S(1)}, bf16[128,1024]{1,0:T(8,128)(2,1)}, u32[]{:S(2)}) copy-start(bf16[128,1024]{1,0:T(8,128)(2,1)} %param.13) | copy-start | bytes 786436
  78.5 24.2 %copy-start.6 = (bf16[1024]{0:T(1024)(128)(2,1)S(1)}, bf16[1024]{0:T(1024)(128)(2,1)}, u32[]{:S(2)}) copy-start(bf16[1024]{0:T(1024)(128)(2,1)} %param.14) | copy-start | bytes 6148
  80.0 47.1 %all-reduce.5.cloned.1.call-start = ((), (), s32[]{:S(2)}) async-start(), calls=%async_computation.7 | async-start | bytes 524288 | tf_op jit(solution)/shard_map/psum | solution.py:105
  99.9 3.8 %copy-start.4 = (bf16[1,128,512]{2,1,0:T(8,128)(2,1)S(1)}, bf16[1,128,512]{2,1,0:T(8,128)(2,1)}, u32[]{:S(2)}) copy-start(bf16[1,128,512]{2,1,0:T(8,128)(2,1)} %reduce-scatter.6.cloned.1.call-done) | copy-start | bytes 393220
  103.6 127.4 %all-reduce.7.cloned.1.call-start = ((), (), s32[]{:S(2)}) async-start(), calls=%async_computation.8 | async-start | bytes 4194304 | tf_op jit(solution)/shard_map/psum | solution.py:108
  105.5 232.7 %reduce-scatter.8.cloned.1.call-start = ((), (), s32[]{:S(2)}) async-start(), calls=%async_computation.9 | async-start | bytes 8912896 | tf_op jit(solution)/shard_map/reduce_scatter | solution.py:58
Sparse Core Ops, SparseCore 0:
  10.1 59.2 all-gather.4
  74.7 10.4 reduce-scatter.9
  88.0 11.7 reduce-scatter.5
  103.7 23.3 all-reduce.4
  131.1 99.8 all-reduce.6
  235.4 102.7 reduce-scatter.7
where the time goes:
time: 349 us; the launch traced here: 348 us
  waiting for transfers between devices  191 us (55%)
  blocking collectives  85.8 us (25%)
  matrix products  20.9 us (6%)
  between operations  16.3 us (5%)
  local copies, waits for them, and re-layouts  16 us (5%)
  starting transfers between devices  13.6 us (4%)
  other arithmetic  4.8 us (1%)
    reduce_scatter x1, waiting for transfers between devices, on_device(): lax.psum_scatter(jnp.einsum('qi,qm->im', output_residual, act_all, prefer...  107 us
    psum x1, blocking collectives, on_device(): lax.psum((weight_mid, bias_mid, hidden_grad, hidden_bgrad), 'dp')  70.9 us
    psum x1, waiting for transfers between devices, on_device(): lax.psum((weight_mid, bias_mid, hidden_grad, hidden_bgrad), 'dp')  33 us
    reduce_scatter x1, waiting for transfers between devices, on_device(): lax.psum_scatter(tan_partial.astype(jnp.bfloat16), 'mp', scatter_dimensio...  13.6 us
    all_gather x1, waiting for transfers between devices, on_device(): decoder_full_rows = lax.all_gather(decoder_weight, 'dp', axis=0, tiled=True)  13.1 us
    psum x1, waiting for transfers between devices, on_device(): lax.psum(weight_part.astype(jnp.bfloat16), 'mp').astype(jnp.float32)  12 us
    all_to_all x1, starting transfers between devices, on_device(): lax.all_to_all(target_window, 'dp', split_axis=0, concat_axis=1, tiled=True)  7.39 us
    gather x1, local copies, waits for them, and re-layouts, on_device(): jac_window = jac_store[window]  7.22 us
  transfers between devices with their start and end apart: 8, of which 7 were waited for; matrix products, arithmetic and copies ran while one was open for 9% of the time, Pallas kernels for 0%

commit v1 on v0

--- a/solution.py
+++ b/solution.py
@@ -2,6 +2,11 @@
 import jax.numpy as jnp
 from jax import lax
 from jax.sharding import PartitionSpec as P
+
+
+def gather_and_add(value, mesh_axis):
+    terms = lax.all_gather(value, mesh_axis)
+    return jnp.sum(terms, axis=0)
 
 
 def on_device(
@@ -102,7 +107,7 @@
     ) + jnp.sum(tan_lower * first_slope[:, None, :], axis=0)
     bias_part = jnp.sum(pre_lower, axis=0)
     weight_mid, bias_mid = (
-        lax.psum(weight_part.astype(jnp.bfloat16), "mp").astype(jnp.float32),
+        gather_and_add(weight_part.astype(jnp.bfloat16), "mp").astype(jnp.float32),
         lax.psum(bias_part.astype(jnp.bfloat16), "mp").astype(jnp.float32),
     )
     first_weights, first_biases, hidden_weights, hidden_biases = lax.psum(

time: 349 us -> 321 us (0.920)
  waiting for transfers between devices: 191 us -> 160 us
  blocking collectives: 85.8 us -> 89.6 us
    psum x1, waiting for transfers between devices: 33 us -> 13.8 us  [on_device(): lax.psum((weight_mid, bias_mid, hidden_grad, hidden_bgrad), 'dp')]
    psum x1 -> x0, waiting for transfers between devices: 12 us -> none  [on_device(): lax.psum(weight_part.astype(jnp.bfloat16), 'mp').astype(jnp.float32)]
    all_gather x0 -> x1, blocking collectives: none -> 7.66 us  [gather_and_add(): terms = lax.all_gather(value, mesh_axis)]
    psum x1, blocking collectives: 70.9 us -> 67 us  [on_device(): lax.psum((weight_mid, bias_mid, hidden_grad, hidden_bgrad), 'dp')]
  transfers between devices with their start and end apart: 8 -> 7, of which waited for: 7 -> 6; matrix products, arithmetic and copies ran while one was open for 9% -> 9% of each run, Pallas kernels for 0% -> 0%
where the time goes in v1:
time: 321 us
  waiting for transfers between devices  160 us (50%)
  blocking collectives  89.6 us (28%)
  matrix products  20.9 us (7%)
  local copies, waits for them, and re-layouts  16 us (5%)
  between operations  15.9 us (5%)
  starting transfers between devices  13.6 us (4%)
  other arithmetic  4.18 us (1%)
    reduce_scatter x1, waiting for transfers between devices, on_device(): lax.psum_scatter(jnp.einsum('qi,qm->im', output_residual, act_all, prefer...  107 us
    psum x1, blocking collectives, on_device(): lax.psum((weight_mid, bias_mid, hidden_grad, hidden_bgrad), 'dp')  67 us
    psum x1, waiting for transfers between devices, on_device(): lax.psum((weight_mid, bias_mid, hidden_grad, hidden_bgrad), 'dp')  13.8 us
    reduce_scatter x1, waiting for transfers between devices, on_device(): lax.psum_scatter(tan_partial.astype(jnp.bfloat16), 'mp', scatter_dimensio...  13.6 us
    all_gather x1, waiting for transfers between devices, on_device(): decoder_full_rows = lax.all_gather(decoder_weight, 'dp', axis=0, tiled=True)  13.1 us
    all_gather x1, blocking collectives, gather_and_add(): terms = lax.all_gather(value, mesh_axis)  7.66 us
    all_to_all x1, starting transfers between devices, on_device(): lax.all_to_all(target_window, 'dp', split_axis=0, concat_axis=1, tiled=True)  7.39 us
    gather x1, local copies, waits for them, and re-layouts, on_device(): jac_window = jac_store[window]  7.22 us
  transfers between devices with their start and end apart: 7, of which 6 were waited for; matrix products, arithmetic and copies ran while one was open for 9% of the time, Pallas kernels for 0%

profile of v1, /device:TPU:0, one launch (start us, length us, event | category | flops | bytes accessed | tf_op | source)
XLA Modules:
  0.0 320.5 jit_solution(7931420647954568272)
XLA Ops:
  8.6 1.5 gather_fusion
  10.7 7.4 %all-to-all-start = ((bf16[16,1,128]{2,1,0:T(2,128)(2,1)}), bf16[16,1,128]{2,1,0:T(2,128)(2,1)S(1)}, u32[]{:S(2)}, u32[]{:S(2)}) async-start(bf16[16,1,128]{2,1,0:T(2,128)(2,1)} %copy.16), calls=%async_computation | async-start | bytes 16384 | tf_op jit(solution)/shard_map/all_to_all | solution.py:28
  18.1 1.2 dynamic_slice.3
  21.3 1.1 fusion.18
  22.4 7.2 %gather_fusion.1 = bf16[16,128,128]{2,1,0:T(8,128)(2,1)} fusion(bf16[512,128,128]{2,1,0:T(8,128)(2,1)} %param.12, s32[1024]{0:T(1024)S(1)} %pad_clamp_fusion), kind=kCustom, calls=%fused_computation.1 | custom fusion | bytes 1048640 | tf_op jit(solution)/shard_map/gather | solution.py:24
  29.6 6.0 %all-to-all-start.1 = ((bf16[16,128,128]{2,1,0:T(8,128)(2,1)}), bf16[16,128,128]{2,1,0:T(8,128)(2,1)S(1)}, u32[]{:S(2)}, u32[]{:S(2)}) async-start(bf16[16,128,128]{2,1,0:T(8,128)(2,1)} %gather_fusion.1), calls=%async_computation.1 | async-start | bytes 1048576 | tf_op jit(solution)/shard_map/all_to_all | solution.py:27
  37.3 4.4 %all-gather.3 = bf16[2,1,512]{2,1,0:T(2,128)(2,1)S(1)} all-gather(bf16[1,1,512]{2,1,0:T(2,128)(2,1)S(1)} %reshape.174), channel_id=2, replica_groups=mesh['dp'=16,'mp'=2] {'mp'}, dimensions={0}, use_global_device_ids=true | all-gather | bytes 3072 | tf_op jit(solution)/shard_map/all_gather | solution.py:51
  41.7 2.0 multiply_convert_fusion
  43.7 5.6 %all-gather.1 = bf16[128,1024]{1,0:T(8,128)(2,1)S(1)} all-gather(bf16[128,512]{1,0:T(8,128)(2,1)S(1)} %get-tuple-element.30), channel_id=3, replica_groups=mesh['dp'=16,'mp'=2] {'mp'}, dimensions={1}, use_global_device_ids=true | all-gather | bytes 393216 | tf_op jit(solution)/shard_map/all_gather | solution.py:52
  49.3 6.6 %all-to-all-done.1 = bf16[16,128,128]{2,1,0:T(8,128)(2,1)S(1)} async-done(((bf16[16,128,128]{2,1,0:T(8,128)(2,1)}), bf16[16,128,128]{2,1,0:T(8,128)(2,1)S(1)}, u32[]{:S(2)}, u32[]{:S(2)}) %all-to-all-start.1) | async-done | bytes 524320 | tf_op jit(solution)/shard_map/all_to_all | solution.py:27
  56.4 13.1 %all-gather.6.cloned.1.call-done = bf16[2048,1024]{1,0:T(8,128)(2,1)} async-done(((bf16[128,1024]{1,0:T(8,128)(2,1)}), bf16[2048,1024]{1,0:T(8,128)(2,1)}) %all-gather.6.cloned.1.call-update) | async-done | bytes 4194320 | tf_op jit(solution)/shard_map/all_gather | solution.py:54
  69.4 3.5 %fusion.26 = f32[1,2048]{1,0:T(1,128)S(1)} fusion(bf16[1024,1]{0,1:T(2,128)(2,1)S(1)} %bitcast.66, bf16[2048,1024]{1,0:T(8,128)(2,1)} %all-gather.6.cloned.1.call-done), kind=kOutput, calls=%fused_computation.48 | convolution fusion | flops 4194304 | bytes 4204544 | tf_op jit(solution)/shard_map/sk,ok->so/dot_general | solution.py:55
  74.6 3.8 %fusion.1 = bf16[2048,128]{0,1:T(8,128)(2,1)S(1)} fusion(f32[2048,128]{0,1:T(8,128)S(1)} %copy.18, bf16[128,1024]{1,0:T(8,128)(2,1)S(1)} %all-gather.1, bf16[2048,1024]{1,0:T(8,128)(2,1)} %all-gather.6.cloned.1.call-done), kind=kOutput, calls=%fused_computation.5 | convolution fusion | flops 537395200 | bytes 6029312 | tf_op jit(solution)/shard_map/mvn,an->mav/dot_general | solution.py:58
  78.5 1.4 fusion.2
  80.1 5.2 %reduce-scatter.10.cloned.1.call-done = bf16[512,1]{1,0:T(8,128)(2,1)} async-done(((bf16[1024,1]{1,0:T(8,128)(2,1)}), bf16[512,1]{1,0:T(8,128)(2,1)}) %reduce-scatter.10.cloned.1.call-update) | async-done | bytes 1040
  86.2 13.6 %reduce-scatter.6.cloned.1.call-done = bf16[1,128,512]{2,1,0:T(8,128)(2,1)} async-done(((bf16[1,128,1024]{2,1,0:T(8,128)(2,1)}), bf16[1,128,512]{2,1,0:T(8,128)(2,1)}) %reduce-scatter.6.cloned.1.call-update) | async-done | bytes 131088 | tf_op jit(solution)/shard_map/reduce_scatter | solution.py:82
  100.9 2.7 multiply_add_fusion.1
  103.7 4.5 %multiply_add_fusion = f32[2048,1024]{1,0:T(8,128)} fusion(bf16[2048,128]{0,1:T(8,128)(2,1)S(1)} %fusion.1, bf16[128,1024]{1,0:T(8,128)(2,1)S(1)} %all-gather.1, f32[1024]{0:T(1024)S(1)} %convert.22, f32[2048]{0:T(1024)S(1)} %get-tuple-element.19), kind=kOutput, calls=%fused_computation.2 | convolution fusion | flops 541065216 | bytes 9187328 | tf_op jit(solution)/shard_map/hzy,hym->zm/dot_general | solution.py:65
  109.9 4.9 %psum.36 = bf16[1024]{0:T(1024)(128)(2,1)S(1)} all-reduce(bf16[1024]{0:T(1024)(128)(2,1)S(1)} %get-tuple-element.25), channel_id=1, replica_groups=mesh['dp'=16,'mp'=2] {'mp'}, use_global_device_ids=true, to_apply=%region_6.0 | all-reduce | flops 1024 | bytes 4096 | tf_op jit(solution)/shard_map/psum | solution.py:111
  115.0 7.7 %all-gather.2 = bf16[256,1024]{1,0:T(8,128)(2,1)S(1)} all-gather(bf16[128,1024]{1,0:T(8,128)(2,1)S(1)} %add_convert_fusion), channel_id=4, replica_groups=mesh['dp'=16,'mp'=2] {'mp'}, dimensions={0}, use_global_device_ids=true | all-gather | bytes 786432 | tf_op jit(solution)/shard_map/all_gather | solution.py:8
  122.7 67.0 %all-reduce.5 = (f32[128,1024]{1,0:T(8,128)}, f32[1024]{0:T(1024)}, f32[512]{0:T(512)}) all-reduce(bf16[128,1024]{1,0:T(8,128)(2,1)S(1)} %reduce_sum.37, bf16[1024]{0:T(1024)(128)(2,1)S(1)} %psum.36, f32[512]{0:T(512)S(1)} %bitcast.69), channel_id=1, replica_groups=mesh['dp'=16,'mp'=2] {'dp'}, use_global_device_ids=true, to_apply=%region_5.0 | all-reduce | flops 132608 | bytes 796672 | tf_op jit(solution)/shard_map/psum | solution.py:113
  189.7 13.8 %all-reduce.4.cloned.1.call-done = f32[1024,512]{1,0:T(8,128)} async-done(((f32[1024,512]{1,0:T(8,128)}), f32[1024,512]{1,0:T(8,128)}) %all-reduce.4.cloned.1.call-update) | async-done | bytes 2097168 | tf_op jit(solution)/shard_map/psum | solution.py:113
  203.6 107.3 %reduce-scatter.8.cloned.1.call-done = f32[128,1024]{1,0:T(8,128)} async-done(((f32[2048,1024]{1,0:T(8,128)}), f32[128,1024]{1,0:T(8,128)}) %reduce-scatter.8.cloned.1.call-update) | async-done | bytes 524304 | tf_op jit(solution)/shard_map/reduce_scatter | solution.py:63
  310.9 3.1 copy.28
  (57 shorter events, 9.8 us)
Async XLA Ops:
  7.2 29.2 %copy-start = (bf16[1024,512]{1,0:T(8,128)(2,1)S(1)}, bf16[1024,512]{1,0:T(8,128)(2,1)}, u32[]{:S(2)}) copy-start(bf16[1024,512]{1,0:T(8,128)(2,1)} %param.15) | copy-start | bytes 3145732
  7.2 62.2 %all-gather.6.cloned.1.call-start = ((), (), s32[]{:S(2)}) async-start(), calls=%async_computation.5 | async-start | bytes 4456448 | tf_op jit(solution)/shard_map/all_gather | solution.py:54
  10.7 18.9 %all-to-all-start = ((bf16[16,1,128]{2,1,0:T(2,128)(2,1)}), bf16[16,1,128]{2,1,0:T(2,128)(2,1)S(1)}, u32[]{:S(2)}, u32[]{:S(2)}) async-start(bf16[16,1,128]{2,1,0:T(2,128)(2,1)} %copy.16), calls=%async_computation | async-start | bytes 16384 | tf_op jit(solution)/shard_map/all_to_all | solution.py:28
  29.6 26.3 %all-to-all-start.1 = ((bf16[16,128,128]{2,1,0:T(8,128)(2,1)}), bf16[16,128,128]{2,1,0:T(8,128)(2,1)S(1)}, u32[]{:S(2)}, u32[]{:S(2)}) async-start(bf16[16,128,128]{2,1,0:T(8,128)(2,1)} %gather_fusion.1), calls=%async_computation.1 | async-start | bytes 1048576 | tf_op jit(solution)/shard_map/all_to_all | solution.py:27
  35.6 49.6 %reduce-scatter.10.cloned.1.call-start = ((), (), s32[]{:S(2)}) async-start(), calls=%async_computation.9 | async-start | bytes 393216
  69.4 3.6 %copy-start.1 = (bf16[2048,1024]{1,0:T(8,128)(2,1)S(1)}, bf16[2048,1024]{1,0:T(8,128)(2,1)}, u32[]{:S(2)}) copy-start(bf16[2048,1024]{1,0:T(8,128)(2,1)} %all-gather.6.cloned.1.call-done) | copy-start | bytes 12582916
  74.6 25.3 %reduce-scatter.6.cloned.1.call-start = ((), (), s32[]{:S(2)}) async-start(), calls=%async_computation.6 | async-start | bytes 393216 | tf_op jit(solution)/shard_map/reduce_scatter | solution.py:82
  74.6 3.9 %copy-start.2 = (bf16[2048,1024]{1,0:T(8,128)(2,1)S(1)}, bf16[2048,1024]{1,0:T(8,128)(2,1)}, u32[]{:S(2)}) copy-start(bf16[2048,1024]{1,0:T(8,128)(2,1)} %all-gather.6.cloned.1.call-done) | copy-start | bytes 12582916
  78.5 21.4 %copy-start.5 = (f32[128,512]{1,0:T(8,128)S(1)}, f32[128,512]{1,0:T(8,128)}, u32[]{:S(2)}) copy-start(f32[128,512]{1,0:T(8,128)} %get-tuple-element.31) | copy-start | bytes 786436
  78.5 22.3 %copy-start.7 = (bf16[512]{0:T(512)(128)(2,1)S(1)}, bf16[512]{0:T(512)(128)(2,1)}, u32[]{:S(2)}) copy-start(bf16[512]{0:T(512)(128)(2,1)} %param.16) | copy-start | bytes 3076
  78.5 22.3 %copy-start.3 = (bf16[128,1024]{1,0:T(8,128)(2,1)S(1)}, bf16[128,1024]{1,0:T(8,128)(2,1)}, u32[]{:S(2)}) copy-start(bf16[128,1024]{1,0:T(8,128)(2,1)} %param.13) | copy-start | bytes 786436
  80.0 123.5 %all-reduce.4.cloned.1.call-start = ((), (), s32[]{:S(2)}) async-start(), calls=%async_computation.7 | async-start | bytes 4194304 | tf_op jit(solution)/shard_map/psum | solution.py:113
  103.6 207.3 %reduce-scatter.8.cloned.1.call-start = ((), (), s32[]{:S(2)}) async-start(), calls=%async_computation.8 | async-start | bytes 8912896 | tf_op jit(solution)/shard_map/reduce_scatter | solution.py:63
  108.2 1.1 copy-start.4
  108.2 1.7 copy-start.6
Sparse Core Ops, SparseCore 0:
  10.1 59.2 all-gather.5
  74.7 10.4 reduce-scatter.9
  88.0 11.7 reduce-scatter.5
  103.8 99.6 all-reduce.3
  208.0 102.8 reduce-scatter.7
